TPU v7x, 32 devices: a whole 2x2x4 slice. The times are simulated.
32 devices in a mesh: px: 8 (over z, y), py: 4 (over x, core).
Axes of the slice: x: 2, y: 2, z: 4, core: 2. Of those that a mesh axis runs over, the one named last changes fastest.
Arguments:
- mode_field: float32 [64, 512, 1024], P(None, 'px', 'py'), may hold values from -1 to 1
- forcing: float32 [64, 512, 1024], P(None, 'px', 'py'), may hold values from -8 to 8
- visc_base: float32 [64, 1024, 512], P('py', 'px'), may hold values from 0.1 to 3
- depth_inverse: float32 [1024, 64, 64], P('py'), may hold values from -1 to 2, as said below
Outputs:
- mode_field_out: float32 [64, 512, 1024], P(None, 'px', 'py')
- residual_norms: float32 [2], replicated
Inputs may be any that keep to these rules, and one draw needn't show every extreme that they name: `depth_inverse`: each matrix has its diagonal between 0.5 and 1.5 and off-diagonal entries of magnitude at most 0.4 / sqrt(64).
All inputs are finite; a program needn't handle non-finite values.
Results may differ from a plain program's by a relative error of at most 0.0001.
Values sent between devices are 32-bit elements; how exact they have to be, the bound alone decides.
A program may use at most 128 MiB of HBM per device.

v0:
```python
import math
import jax
import jax.numpy as jnp
from jax import lax
from jax.sharding import PartitionSpec as P

ITERS = 2


def depth_tables(count):
    index = jnp.arange(count, dtype=jnp.float32)
    angle = jnp.pi * index[:, None] * index[None, :] / (count - 1)
    ends = jnp.where((index == 0) | (index == count - 1), 2.0, 1.0)
    forward = jnp.cos(angle)
    backward = 2.0 / (count - 1) * jnp.cos(angle) / (ends[:, None] * ends[None, :])
    return (forward, backward)


def hartley_table(count):
    index = jnp.arange(count, dtype=jnp.int32)
    phase = index[:, None] * index[None, :] % count
    angle = phase.astype(jnp.float32) * (2.0 * math.pi / count)
    return (jnp.cos(angle) + jnp.sin(angle)) / math.sqrt(count)


def wave_square(index, count):
    folded = jnp.minimum(index, count - index).astype(jnp.float32)
    scaled = 2.0 * jnp.pi * folded / count
    return scaled * scaled


def local(mode_field, forcing, visc_base, depth_inverse):
    depth_count = mode_field.shape[0]
    rows_y = mode_field.shape[1]
    cols_x = mode_field.shape[2]
    total_y = rows_y * lax.axis_size("px")
    total_x = cols_x * lax.axis_size("py")
    cell_total = depth_count * total_y * total_x
    forward, backward = depth_tables(depth_count)
    table_x = hartley_table(total_x)
    table_y = hartley_table(total_y)
    index_y = lax.axis_index("px") * rows_y + jnp.arange(rows_y, dtype=jnp.int32)
    index_x = lax.axis_index("py") * cols_x + jnp.arange(cols_x, dtype=jnp.int32)
    lateral = wave_square(index_y, total_y)[:, None] + wave_square(index_x, total_x)[None, :]
    highest = lax.Precision.HIGHEST
    field = mode_field
    partials = []
    for sweep in range(ITERS):
        points = jnp.einsum("jm,myx->jyx", forward, field, precision=highest)
        lines = lax.all_to_all(points, "py", split_axis=0, concat_axis=2, tiled=True)
        lines = jnp.einsum("zyk,xk->zyx", lines, table_x, precision=highest)
        columns = lax.all_to_all(lines, "px", split_axis=2, concat_axis=1, tiled=True)
        physical = jnp.einsum("zkx,yk->zxy", columns, table_y, precision=highest)
        stress = visc_base * jnp.power(1.0 + physical * physical, -1.0 / 3.0) * physical
        returned = jnp.einsum("zxy,ky->zkx", stress, table_y, precision=highest)
        returned = lax.all_to_all(returned, "px", split_axis=1, concat_axis=2, tiled=True)
        returned = jnp.einsum("zyx,kx->zyk", returned, table_x, precision=highest)
        spectral = lax.all_to_all(returned, "py", split_axis=2, concat_axis=0, tiled=True)
        viscous = jnp.einsum("mj,jyx->myx", backward, spectral, precision=highest)
        residual = forcing - (lateral * field + viscous)
        squares = jnp.sum(residual * residual)
        partials.append(squares)
        correction = jnp.einsum("xmn,nyx->myx", depth_inverse, residual, precision=highest)
        field = field + correction / (1.0 + lateral)
    norm_values = lax.psum(jnp.stack(partials), ("px", "py")) / cell_total
    return (field, norm_values)


def solution(mesh):
    placed = (P(None, "px", "py"), P(None, "px", "py"), P("py", "px", None), P("py", None, None))
    return jax.shard_map(
        local, mesh=mesh, in_specs=placed, out_specs=(P(None, "px", "py"), P()), check_vma=False
    )
```

profile of v0, /device:TPU:0, one launch (start us, length us, event | category | flops | bytes accessed | tf_op | source)
XLA Modules:
  0.0 1180.5 jit_solution(4981128345261432026)
XLA Ops:
  18.6 17.7 %fusion.151 = f32[1024,1024,1]{1,0,2:T(8,128)} fusion(), kind=kLoop, calls=%fused_computation.17.clone | loop fusion | flops 16777216 | bytes 4194304 | tf_op jit(solution)/shard_map/zyk,xk->zyx/dot_general | solution.py:51
  36.3 31.2 %all-to-all-done = f32[64,64,256]{2,1,0:T(8,128)} async-done(((f32[64,64,256]{2,1,0:T(8,128)}), f32[64,64,256]{2,1,0:T(8,128)}, u32[]{:S(2)}, u32[]{:S(2)}) %all-to-all-start) | async-done | bytes 4194336 | tf_op jit(solution)/shard_map/all_to_all | solution.py:50
  80.3 17.6 %fusion.11 = f32[16,64,1024]{2,1,0:T(8,128)} fusion(f32[16,64,1024]{2,1,0:T(8,128)} %all_to_all.107, f32[1024,1024,1]{1,0,2:T(8,128)} %fusion.151), kind=kOutput, calls=%fused_computation.16 | convolution fusion | flops 12884901888 | bytes 12582912 | tf_op jit(solution)/shard_map/zyk,xk->zyx/dot_general | solution.py:51
  106.1 9.8 reshape.101
  115.9 99.8 %all_to_all.144 = f32[8,1,131072]{2,1,0:T(1,128)} all-to-all(f32[8,1,131072]{2,1,0:T(1,128)} %reshape.101), channel_id=1, replica_groups=mesh['px'=8,'py'=4] {'px'}, dimensions={0} | all-to-all | bytes 8388608 | tf_op jit(solution)/shard_map/all_to_all | solution.py:52
  216.2 13.8 %reduce = f32[8,131072]{1,0:T(8,128)} reduce(f32[8,1,131072]{2,1,0:T(1,128)} %all_to_all.144, f32[]{:T(128)} %broadcast.189), dimensions={1}, to_apply=%all_to_all.108.reduce_sub_computation | reduce | bytes 8388612 | tf_op jit(solution)/shard_map/all_to_all | solution.py:52
  245.9 19.7 %fusion.47 = f32[16,128,512]{2,1,0:T(8,128)S(1)} fusion(f32[16,512,128]{2,1,0:T(8,128)} %bitcast.126), kind=kOutput, calls=%fused_computation.60 | convolution fusion | flops 6446645248 | bytes 8388608 | tf_op jit(solution)/shard_map/zkx,yk->zxy/dot_general | solution.py:53
  265.6 16.7 %fusion.30 = f32[16,512,128]{2,1,0:T(8,128)S(1)} fusion(f32[16,128,512]{2,1,0:T(8,128)S(1)} %fusion.47, f32[16,128,512]{2,1,0:T(8,128)S(1)} %copy-done.1), kind=kOutput, calls=%fused_computation.44 | convolution fusion | flops 6450839552 | bytes 12582912 | tf_op jit(solution)/shard_map/zxy,ky->zkx/dot_general | solution.py:55
  291.5 17.7 %fusion.149 = f32[1024,1024,1]{1,0,2:T(8,128)} fusion(), kind=kLoop, calls=%fused_computation.15.clone | loop fusion | flops 16777216 | bytes 4194304 | tf_op jit(solution)/shard_map/zyx,kx->zyk/dot_general | solution.py:57
  309.2 74.6 %all-to-all-done.2 = f32[16,512,128]{2,0,1:T(8,128)} async-done(((f32[16,512,128]{2,0,1:T(8,128)}), f32[16,512,128]{2,0,1:T(8,128)}, u32[]{:S(2)}, u32[]{:S(2)}) %all-to-all-start.2) | async-done | bytes 4194336 | tf_op jit(solution)/shard_map/all_to_all | solution.py:56
  395.3 17.6 %fusion.9 = f32[16,64,1024]{2,1,0:T(8,128)} fusion(f32[16,64,1024]{2,1,0:T(8,128)} %all_to_all.115, f32[1024,1024,1]{1,0,2:T(8,128)} %fusion.149), kind=kOutput, calls=%fused_computation.14 | convolution fusion | flops 12884901888 | bytes 12582912 | tf_op jit(solution)/shard_map/zyx,kx->zyk/dot_general | solution.py:57
  443.9 38.9 %all-to-all-done.3 = f32[4,1,262144]{2,1,0:T(1,128)} async-done(((f32[4,1,262144]{2,1,0:T(1,128)}), f32[4,1,262144]{2,1,0:T(1,128)}, u32[]{:S(2)}, u32[]{:S(2)}) %all-to-all-start.3) | async-done | bytes 4194336 | tf_op jit(solution)/shard_map/all_to_all | solution.py:58
  482.9 15.3 %reduce.1 = f32[4,262144]{1,0:T(4,128)} reduce(f32[4,1,262144]{2,1,0:T(1,128)} %all-to-all-done.3, f32[]{:T(128)} %broadcast.189), dimensions={1}, to_apply=%all_to_all.116.reduce_sub_computation | reduce | bytes 8388612 | tf_op jit(solution)/shard_map/all_to_all | solution.py:58
  498.2 9.2 reshape.104
  516.3 15.4 %multiply_reduce_fusion.1 = (f32[]{:T(128)}, f32[64,64,256]{2,0,1:T(8,128)}) fusion(f32[64,64,256]{2,0,1:T(8,128)} %bitcast.125, f32[64]{0:T(128)S(1)} %get-tuple-element.16, f32[64]{0:T(128)S(1)} %get-tuple-element.17, f32[64,64,256]{2,1,0:T(8,128)} %param.4, f32[64,256]{1,0:T(8,128)S(1)} %get-tuple-element.11, f32[64,64,256]{2,1,0:T(8,128)} %param.5), kind=kOutput, calls=%fused_computation.23 | convolution fusion | flops 810569728 | bytes 16843268 | tf_op jit(solution)/shard_map/mj,jyx->myx/dot_general | solution.py:59
  540.9 19.3 %fusion.127 = f32[256,64,64]{2,1,0:T(8,128)} fusion(f32[64,64,256]{0,1,2:T(8,128)} %copy.89, f32[256,64,64]{2,1,0:T(8,128)} %copy.90), kind=kOutput, calls=%fused_computation.151 | convolution fusion | flops 805306368 | bytes 12582912 | tf_op jit(solution)/shard_map/xmn,nyx->myx/dot_general | solution.py:63
  588.0 17.7 %fusion.147 = f32[1024,1024,1]{1,0,2:T(8,128)} fusion(), kind=kLoop, calls=%fused_computation.13.clone | loop fusion | flops 16777216 | bytes 4194304 | tf_op jit(solution)/shard_map/zyk,xk->zyx/dot_general | solution.py:51
  605.7 30.5 %all-to-all-done.4 = f32[64,64,256]{2,1,0:T(8,128)} async-done(((f32[64,64,256]{2,1,0:T(8,128)}), f32[64,64,256]{2,1,0:T(8,128)}, u32[]{:S(2)}, u32[]{:S(2)}) %all-to-all-start.4) | async-done | bytes 4194336 | tf_op jit(solution)/shard_map/all_to_all | solution.py:50
  648.9 17.6 %fusion.7 = f32[16,64,1024]{2,1,0:T(8,128)} fusion(f32[16,64,1024]{2,1,0:T(8,128)} %all_to_all.123, f32[1024,1024,1]{1,0,2:T(8,128)} %fusion.147), kind=kOutput, calls=%fused_computation.12 | convolution fusion | flops 12884901888 | bytes 12582912 | tf_op jit(solution)/shard_map/zyk,xk->zyx/dot_general | solution.py:51
  674.7 9.8 reshape.105
  684.5 97.7 %all_to_all.145 = f32[8,1,131072]{2,1,0:T(1,128)} all-to-all(f32[8,1,131072]{2,1,0:T(1,128)} %reshape.105), channel_id=1, replica_groups=mesh['px'=8,'py'=4] {'px'}, dimensions={0} | all-to-all | bytes 8388608 | tf_op jit(solution)/shard_map/all_to_all | solution.py:52
  782.2 13.7 %reduce.2 = f32[8,131072]{1,0:T(8,128)} reduce(f32[8,1,131072]{2,1,0:T(1,128)} %all_to_all.145, f32[]{:T(128)} %broadcast.189), dimensions={1}, to_apply=%all_to_all.124.reduce_sub_computation | reduce | bytes 8388612 | tf_op jit(solution)/shard_map/all_to_all | solution.py:52
  811.5 19.9 %fusion.44 = f32[16,128,512]{2,1,0:T(8,128)S(1)} fusion(f32[16,512,128]{2,1,0:T(8,128)} %bitcast.127), kind=kOutput, calls=%fused_computation.57 | convolution fusion | flops 6446645248 | bytes 8388608 | tf_op jit(solution)/shard_map/zkx,yk->zxy/dot_general | solution.py:53
  831.5 16.5 %fusion.33 = f32[16,512,128]{2,1,0:T(8,128)S(1)} fusion(f32[16,128,512]{2,1,0:T(8,128)S(1)} %fusion.44, f32[16,128,512]{2,1,0:T(8,128)S(1)} %copy-done.2), kind=kOutput, calls=%fused_computation.45 | convolution fusion | flops 6450839552 | bytes 12582912 | tf_op jit(solution)/shard_map/zxy,ky->zkx/dot_general | solution.py:55
  857.3 17.7 %fusion.145 = f32[1024,1024,1]{1,0,2:T(8,128)} fusion(), kind=kLoop, calls=%fused_computation.11.clone.1 | loop fusion | flops 16777216 | bytes 4194304 | tf_op jit(solution)/shard_map/zyx,kx->zyk/dot_general | solution.py:57
  875.0 74.6 %all-to-all-done.6 = f32[16,512,128]{2,0,1:T(8,128)} async-done(((f32[16,512,128]{2,0,1:T(8,128)}), f32[16,512,128]{2,0,1:T(8,128)}, u32[]{:S(2)}, u32[]{:S(2)}) %all-to-all-start.6) | async-done | bytes 4194336 | tf_op jit(solution)/shard_map/all_to_all | solution.py:56
  961.0 17.6 %fusion.5 = f32[16,64,1024]{2,1,0:T(8,128)} fusion(f32[16,64,1024]{2,1,0:T(8,128)} %all_to_all.131, f32[1024,1024,1]{1,0,2:T(8,128)} %fusion.145), kind=kOutput, calls=%fused_computation.10 | convolution fusion | flops 12884901888 | bytes 12582912 | tf_op jit(solution)/shard_map/zyx,kx->zyk/dot_general | solution.py:57
  995.5 53.9 %all_to_all.146 = f32[4,1,262144]{2,1,0:T(1,128)} all-to-all(f32[4,1,262144]{2,1,0:T(1,128)} %reshape.107), channel_id=1, replica_groups=mesh['px'=8,'py'=4] {'py'}, dimensions={0} | all-to-all | bytes 8388608 | tf_op jit(solution)/shard_map/all_to_all | solution.py:58
  1049.3 15.2 %reduce.3 = f32[4,262144]{1,0:T(4,128)} reduce(f32[4,1,262144]{2,1,0:T(1,128)} %all_to_all.146, f32[]{:T(128)} %broadcast.189), dimensions={1}, to_apply=%all_to_all.132.reduce_sub_computation | reduce | bytes 8388612 | tf_op jit(solution)/shard_map/all_to_all | solution.py:58
  1082.3 13.4 %multiply_reduce_fusion = (f32[]{:T(128)}, f32[64,64,256]{2,0,1:T(8,128)}) fusion(f32[64,64,256]{2,0,1:T(8,128)} %bitcast.124, f32[64]{0:T(128)S(1)} %get-tuple-element.16, f32[64]{0:T(128)S(1)} %get-tuple-element.17, f32[64,64,256]{2,0,1:T(8,128)} %copy-done, f32[64,256]{1,0:T(8,128)S(1)} %get-tuple-element.11, f32[64,64,256]{2,1,0:T(8,128)} %param.5), kind=kOutput, calls=%fused_computation.22 | convolution fusion | flops 810569728 | bytes 16843268 | tf_op jit(solution)/shard_map/mj,jyx->myx/dot_general | solution.py:59
  1104.8 19.4 %fusion.128 = f32[256,64,64]{2,1,0:T(8,128)} fusion(f32[64,64,256]{0,1,2:T(8,128)} %copy.104, f32[256,64,64]{2,1,0:T(8,128)} %copy.90), kind=kOutput, calls=%fused_computation.152 | convolution fusion | flops 805306368 | bytes 12582912 | tf_op jit(solution)/shard_map/xmn,nyx->myx/dot_general | solution.py:63
  1142.2 37.5 %psum.7 = f32[2]{0:T(128)S(1)} all-reduce(f32[2]{0:T(128)S(1)} %pad_maximum_fusion), channel_id=1, replica_groups=mesh['px'=8,'py'=4] {'px','py'}, use_global_device_ids=true, to_apply=%region_2.3 | all-reduce | flops 2 | bytes 16 | tf_op jit(solution)/shard_map/psum | solution.py:65
  (53 shorter events, 272.6 us)
Async XLA Ops:
  13.6 53.9 %all-to-all-start = ((f32[64,64,256]{2,1,0:T(8,128)}), f32[64,64,256]{2,1,0:T(8,128)}, u32[]{:S(2)}, u32[]{:S(2)}) async-start(f32[64,64,256]{2,1,0:T(8,128)} %copy.78), calls=%async_computation | async-start | bytes 8388608 | tf_op jit(solution)/shard_map/all_to_all | solution.py:50
  245.9 19.7 %copy-start.1 = (f32[16,128,512]{2,1,0:T(8,128)S(1)}, f32[16,128,512]{2,1,0:T(8,128)}, u32[]{:S(2)}) copy-start(f32[16,128,512]{2,1,0:T(8,128)} %param.6) | copy-start | bytes 12582916
  286.9 96.8 %all-to-all-start.2 = ((f32[16,512,128]{2,0,1:T(8,128)}), f32[16,512,128]{2,0,1:T(8,128)}, u32[]{:S(2)}, u32[]{:S(2)}) async-start(f32[16,512,128]{2,0,1:T(8,128)} %copy.84), calls=%async_computation.2 | async-start | bytes 8388608 | tf_op jit(solution)/shard_map/all_to_all | solution.py:56
  429.7 53.1 %all-to-all-start.3 = ((f32[4,1,262144]{2,1,0:T(1,128)}), f32[4,1,262144]{2,1,0:T(1,128)}, u32[]{:S(2)}, u32[]{:S(2)}) async-start(f32[4,1,262144]{2,1,0:T(1,128)} %reshape.103), calls=%async_computation.3 | async-start | bytes 8388608 | tf_op jit(solution)/shard_map/all_to_all | solution.py:58
  574.3 4.0 copy-start
  582.7 53.5 %all-to-all-start.4 = ((f32[64,64,256]{2,1,0:T(8,128)}), f32[64,64,256]{2,1,0:T(8,128)}, u32[]{:S(2)}, u32[]{:S(2)}) async-start(f32[64,64,256]{2,1,0:T(8,128)} %copy.93), calls=%async_computation.4 | async-start | bytes 8388608 | tf_op jit(solution)/shard_map/all_to_all | solution.py:50
  811.5 19.9 %copy-start.2 = (f32[16,128,512]{2,1,0:T(8,128)S(1)}, f32[16,128,512]{2,1,0:T(8,128)}, u32[]{:S(2)}) copy-start(f32[16,128,512]{2,1,0:T(8,128)} %param.6) | copy-start | bytes 12582916
  852.7 96.9 %all-to-all-start.6 = ((f32[16,512,128]{2,0,1:T(8,128)}), f32[16,512,128]{2,0,1:T(8,128)}, u32[]{:S(2)}, u32[]{:S(2)}) async-start(f32[16,512,128]{2,0,1:T(8,128)} %copy.99), calls=%async_computation.6 | async-start | bytes 8388608 | tf_op jit(solution)/shard_map/all_to_all | solution.py:56
where the time goes:
time: 1190 us; the launch traced here: 1180 us
  blocking collectives  289 us (24%)
  local copies, waits for them, and re-layouts  252 us (21%)
  waiting for transfers between devices  250 us (21%)
  matrix products  223 us (19%)
  other arithmetic  141 us (12%)
  starting transfers between devices  24.4 us (2%)
    all_to_all x2, blocking collectives, local(): lax.all_to_all(lines, 'px', split_axis=2, concat_axis=1, tiled=True)  197 us
    all_to_all x2, waiting for transfers between devices, local(): lax.all_to_all(returned, 'px', split_axis=1, concat_axis=2, tiled=True)  149 us
    unnamed x16, local copies, waits for them, and re-layouts  86.7 us
    all_to_all x2, waiting for transfers between devices, local(): lax.all_to_all(points, 'py', split_axis=0, concat_axis=2, tiled=True)  61.6 us
    all_to_all x1, blocking collectives, local(): lax.all_to_all(returned, 'py', split_axis=2, concat_axis=0, tiled=True)  53.9 us
    dot_general x2, matrix products, local(): physical = jnp.einsum('zkx,yk->zxy', columns, table_y, precision=highest)  39.6 us
    all_to_all x1, waiting for transfers between devices, local(): lax.all_to_all(returned, 'py', split_axis=2, concat_axis=0, tiled=True)  38.9 us
    dot_general x2, matrix products, local(): jnp.einsum('xmn,nyx->myx', depth_inverse, residual, precision=highest)  38.7 us
  transfers between devices with their start and end apart: 5, of which 5 were waited for; matrix products, arithmetic and copies ran while one was open for 7% of the time, Pallas kernels for 0%

commit v1 on v0

--- a/solution.py
+++ b/solution.py
@@ -55,7 +55,9 @@
         returned = jnp.einsum("zxy,ky->zkx", stress, table_y, precision=highest)
         returned = lax.all_to_all(returned, "px", split_axis=1, concat_axis=2, tiled=True)
         returned = jnp.einsum("zyx,kx->zyk", returned, table_x, precision=highest)
-        spectral = lax.all_to_all(returned, "py", split_axis=2, concat_axis=0, tiled=True)
+        shards = jnp.split(returned, lax.axis_size("py"), axis=2)
+        received = lax.all_to_all(jnp.stack(shards), "py", 0, 0)
+        spectral = jnp.concatenate(received, axis=0)
         viscous = jnp.einsum("mj,jyx->myx", backward, spectral, precision=highest)
         residual = forcing - (lateral * field + viscous)
         squares = jnp.sum(residual * residual)

time: 1190 us -> 1090 us (0.916)
  local copies, waits for them, and re-layouts: 252 us -> 184 us
  other arithmetic: 141 us -> 114 us
    unnamed x16, local copies, waits for them, and re-layouts: 86.7 us -> 50.6 us
    all_to_all x2 -> x0, other arithmetic: 30.5 us -> none  [local(): lax.all_to_all(returned, 'py', split_axis=2, concat_axis=0, tiled=True)]
    all_to_all x2 -> x0, local copies, waits for them, and re-layouts: 17.4 us -> none  [local(): lax.all_to_all(returned, 'py', split_axis=2, concat_axis=0, tiled=True)]
    dot_general x2 -> x0, local copies, waits for them, and re-layouts: 16.2 us -> none  [local(): returned = jnp.einsum('zyx,kx->zyk', returned, table_x, precision=highest)]
where the time goes in v1:
time: 1090 us; the launch traced here: 1080 us
  blocking collectives  286 us (26%)
  waiting for transfers between devices  250 us (23%)
  matrix products  220 us (20%)
  local copies, waits for them, and re-layouts  184 us (17%)
  other arithmetic  114 us (10%)
  starting transfers between devices  24.4 us (2%)
    all_to_all x2, blocking collectives, local(): lax.all_to_all(lines, 'px', split_axis=2, concat_axis=1, tiled=True)  197 us
    all_to_all x2, waiting for transfers between devices, local(): lax.all_to_all(returned, 'px', split_axis=1, concat_axis=2, tiled=True)  149 us
    all_to_all x2, waiting for transfers between devices, local(): lax.all_to_all(points, 'py', split_axis=0, concat_axis=2, tiled=True)  61.7 us
    all_to_all x1, blocking collectives, local(): received = lax.all_to_all(jnp.stack(shards), 'py', 0, 0)  51.3 us
    unnamed x16, local copies, waits for them, and re-layouts  50.6 us
    dot_general x2, matrix products, local(): physical = jnp.einsum('zkx,yk->zxy', columns, table_y, precision=highest)  39.5 us
    all_to_all x1, waiting for transfers between devices, local(): received = lax.all_to_all(jnp.stack(shards), 'py', 0, 0)  38.9 us
    dot_general x2, matrix products, local(): jnp.einsum('xmn,nyx->myx', depth_inverse, residual, precision=highest)  38.3 us
  transfers between devices with their start and end apart: 5, of which 5 were waited for; matrix products, arithmetic and copies ran while one was open for 7% of the time, Pallas kernels for 0%

profile of v1, /device:TPU:0, one launch (start us, length us, event | category | flops | bytes accessed | tf_op | source)
XLA Modules:
  0.0 1079.8 jit_solution(10654087167274354473)
XLA Ops:
  18.7 17.7 %fusion.157 = f32[1024,1024,1]{1,0,2:T(8,128)} fusion(), kind=kLoop, calls=%fused_computation.19.clone | loop fusion | flops 16777216 | bytes 4194304 | tf_op jit(solution)/shard_map/zyk,xk->zyx/dot_general | solution.py:51
  36.3 31.2 %all-to-all-done = f32[64,64,256]{2,1,0:T(8,128)} async-done(((f32[64,64,256]{2,1,0:T(8,128)}), f32[64,64,256]{2,1,0:T(8,128)}, u32[]{:S(2)}, u32[]{:S(2)}) %all-to-all-start) | async-done | bytes 4194336 | tf_op jit(solution)/shard_map/all_to_all | solution.py:50
  80.4 17.6 %fusion.11 = f32[16,64,1024]{2,1,0:T(8,128)} fusion(f32[16,64,1024]{2,1,0:T(8,128)} %all_to_all.87, f32[1024,1024,1]{1,0,2:T(8,128)} %fusion.157), kind=kOutput, calls=%fused_computation.18 | convolution fusion | flops 12884901888 | bytes 12582912 | tf_op jit(solution)/shard_map/zyk,xk->zyx/dot_general | solution.py:51
  106.4 9.8 reshape.109
  116.2 99.8 %all_to_all.118 = f32[8,1,131072]{2,1,0:T(1,128)} all-to-all(f32[8,1,131072]{2,1,0:T(1,128)} %reshape.109), channel_id=1, replica_groups=mesh['px'=8,'py'=4] {'px'}, dimensions={0} | all-to-all | bytes 8388608 | tf_op jit(solution)/shard_map/all_to_all | solution.py:52
  216.5 13.8 %reduce = f32[8,131072]{1,0:T(8,128)} reduce(f32[8,1,131072]{2,1,0:T(1,128)} %all_to_all.118, f32[]{:T(128)} %broadcast.189), dimensions={1}, to_apply=%all_to_all.88.reduce_sub_computation | reduce | bytes 8388612 | tf_op jit(solution)/shard_map/all_to_all | solution.py:52
  245.9 19.7 %fusion.55 = f32[16,128,512]{2,1,0:T(8,128)S(1)} fusion(f32[16,512,128]{2,1,0:T(8,128)} %bitcast.125), kind=kOutput, calls=%fused_computation.74 | convolution fusion | flops 6446645248 | bytes 8388608 | tf_op jit(solution)/shard_map/zkx,yk->zxy/dot_general | solution.py:53
  265.7 16.8 %fusion.34 = f32[16,512,128]{2,1,0:T(8,128)S(1)} fusion(f32[16,128,512]{2,1,0:T(8,128)S(1)} %fusion.55, f32[16,128,512]{2,1,0:T(8,128)S(1)} %copy-done.2), kind=kOutput, calls=%fused_computation.50 | convolution fusion | flops 6450839552 | bytes 12582912 | tf_op jit(solution)/shard_map/zxy,ky->zkx/dot_general | solution.py:55
  291.7 17.7 %fusion.155 = f32[1024,1024,1]{1,0,2:T(8,128)} fusion(), kind=kLoop, calls=%fused_computation.17.clone | loop fusion | flops 16777216 | bytes 4194304 | tf_op jit(solution)/shard_map/zyx,kx->zyk/dot_general | solution.py:57
  309.3 74.6 %all-to-all-done.2 = f32[16,512,128]{2,0,1:T(8,128)} async-done(((f32[16,512,128]{2,0,1:T(8,128)}), f32[16,512,128]{2,0,1:T(8,128)}, u32[]{:S(2)}, u32[]{:S(2)}) %all-to-all-start.2) | async-done | bytes 4194336 | tf_op jit(solution)/shard_map/all_to_all | solution.py:56
  395.5 16.9 %fusion.9 = f32[16,64,1024]{2,1,0:T(8,128)S(1)} fusion(f32[16,64,1024]{2,1,0:T(8,128)} %all_to_all.95, f32[1024,1024,1]{1,0,2:T(8,128)} %fusion.155), kind=kOutput, calls=%fused_computation.16 | convolution fusion | flops 12884901888 | bytes 12582912 | tf_op jit(solution)/shard_map/zyx,kx->zyk/dot_general | solution.py:57
  420.6 9.2 copy.87
  429.9 38.9 %all-to-all-done.3 = f32[4,16,64,256]{3,2,1,0:T(8,128)} async-done(((f32[4,16,64,256]{3,2,1,0:T(8,128)}), f32[4,16,64,256]{3,2,1,0:T(8,128)}, u32[]{:S(2)}, u32[]{:S(2)}) %all-to-all-start.3) | async-done | bytes 4194336 | tf_op jit(solution)/shard_map/all_to_all | solution.py:59
  468.8 17.3 %multiply_reduce_fusion.1 = (f32[]{:T(128)}, f32[64,64,256]{2,0,1:T(8,128)}) fusion(f32[64,64,256]{2,1,0:T(8,128)} %bitcast.17, f32[64]{0:T(128)S(1)} %or_select_fusion, f32[64]{0:T(128)S(1)} %iota_multiply_fusion, f32[64,64,256]{2,1,0:T(8,128)} %param.4, f32[64,256]{1,0:T(8,128)S(1)} %get-tuple-element.19, f32[64,64,256]{2,1,0:T(8,128)} %param.5), kind=kOutput, calls=%fused_computation.29 | convolution fusion | flops 810569728 | bytes 16843268 | tf_op jit(solution)/shard_map/mj,jyx->myx/dot_general | solution.py:61
  486.1 9.5 copy.86
  495.6 19.2 %fusion.135 = f32[256,64,64]{2,1,0:T(8,128)} fusion(f32[64,64,256]{0,1,2:T(8,128)} %copy.86, f32[256,64,64]{2,1,0:T(8,128)} %copy.87), kind=kOutput, calls=%fused_computation.165 | convolution fusion | flops 805306368 | bytes 12582912 | tf_op jit(solution)/shard_map/xmn,nyx->myx/dot_general | solution.py:65
  542.3 17.7 %fusion.153 = f32[1024,1024,1]{1,0,2:T(8,128)} fusion(), kind=kLoop, calls=%fused_computation.15.clone | loop fusion | flops 16777216 | bytes 4194304 | tf_op jit(solution)/shard_map/zyk,xk->zyx/dot_general | solution.py:51
  560.0 30.5 %all-to-all-done.4 = f32[64,64,256]{2,1,0:T(8,128)} async-done(((f32[64,64,256]{2,1,0:T(8,128)}), f32[64,64,256]{2,1,0:T(8,128)}, u32[]{:S(2)}, u32[]{:S(2)}) %all-to-all-start.4) | async-done | bytes 4194336 | tf_op jit(solution)/shard_map/all_to_all | solution.py:50
  603.2 17.6 %fusion.7 = f32[16,64,1024]{2,1,0:T(8,128)} fusion(f32[16,64,1024]{2,1,0:T(8,128)} %all_to_all.100, f32[1024,1024,1]{1,0,2:T(8,128)} %fusion.153), kind=kOutput, calls=%fused_computation.14 | convolution fusion | flops 12884901888 | bytes 12582912 | tf_op jit(solution)/shard_map/zyk,xk->zyx/dot_general | solution.py:51
  629.2 9.8 reshape.111
  639.0 97.7 %all_to_all.119 = f32[8,1,131072]{2,1,0:T(1,128)} all-to-all(f32[8,1,131072]{2,1,0:T(1,128)} %reshape.111), channel_id=1, replica_groups=mesh['px'=8,'py'=4] {'px'}, dimensions={0} | all-to-all | bytes 8388608 | tf_op jit(solution)/shard_map/all_to_all | solution.py:52
  736.7 13.7 %reduce.1 = f32[8,131072]{1,0:T(8,128)} reduce(f32[8,1,131072]{2,1,0:T(1,128)} %all_to_all.119, f32[]{:T(128)} %broadcast.189), dimensions={1}, to_apply=%all_to_all.101.reduce_sub_computation | reduce | bytes 8388612 | tf_op jit(solution)/shard_map/all_to_all | solution.py:52
  766.0 19.7 %fusion.52 = f32[16,128,512]{2,1,0:T(8,128)S(1)} fusion(f32[16,512,128]{2,1,0:T(8,128)} %bitcast.126), kind=kOutput, calls=%fused_computation.71 | convolution fusion | flops 6446645248 | bytes 8388608 | tf_op jit(solution)/shard_map/zkx,yk->zxy/dot_general | solution.py:53
  785.7 16.8 %fusion.37 = f32[16,512,128]{2,1,0:T(8,128)S(1)} fusion(f32[16,128,512]{2,1,0:T(8,128)S(1)} %fusion.52, f32[16,128,512]{2,1,0:T(8,128)S(1)} %copy-done.3), kind=kOutput, calls=%fused_computation.51 | convolution fusion | flops 6450839552 | bytes 12582912 | tf_op jit(solution)/shard_map/zxy,ky->zkx/dot_general | solution.py:55
  811.6 17.7 %fusion.151 = f32[1024,1024,1]{1,0,2:T(8,128)} fusion(), kind=kLoop, calls=%fused_computation.13.clone.1 | loop fusion | flops 16777216 | bytes 4194304 | tf_op jit(solution)/shard_map/zyx,kx->zyk/dot_general | solution.py:57
  829.3 74.6 %all-to-all-done.6 = f32[16,512,128]{2,0,1:T(8,128)} async-done(((f32[16,512,128]{2,0,1:T(8,128)}), f32[16,512,128]{2,0,1:T(8,128)}, u32[]{:S(2)}, u32[]{:S(2)}) %all-to-all-start.6) | async-done | bytes 4194336 | tf_op jit(solution)/shard_map/all_to_all | solution.py:56
  915.4 16.9 %fusion.5 = f32[16,64,1024]{2,1,0:T(8,128)S(1)} fusion(f32[16,64,1024]{2,1,0:T(8,128)} %all_to_all.108, f32[1024,1024,1]{1,0,2:T(8,128)} %fusion.151), kind=kOutput, calls=%fused_computation.12 | convolution fusion | flops 12884901888 | bytes 12582912 | tf_op jit(solution)/shard_map/zyx,kx->zyk/dot_general | solution.py:57
  933.2 51.3 %all_to_all.120 = f32[4,16,64,256]{3,2,1,0:T(8,128)S(1)} all-to-all(f32[4,16,64,256]{3,2,1,0:T(8,128)S(1)} %pad_maximum_fusion.1), channel_id=1, replica_groups=mesh['px'=8,'py'=4] {'py'}, dimensions={0} | all-to-all | bytes 8388608 | tf_op jit(solution)/shard_map/all_to_all | solution.py:59
  984.5 10.2 multiply_reduce_fusion
  996.0 37.5 %psum.7 = f32[2]{0:T(128)S(1)} all-reduce(f32[2]{0:T(128)S(1)} %pad_maximum_fusion.2), channel_id=1, replica_groups=mesh['px'=8,'py'=4] {'px','py'}, use_global_device_ids=true, to_apply=%region_2.3 | all-reduce | flops 2 | bytes 16 | tf_op jit(solution)/shard_map/psum | solution.py:67
  1034.1 9.1 copy.100
  1043.2 19.2 %fusion.136 = f32[256,64,64]{2,1,0:T(8,128)} fusion(f32[64,64,256]{0,1,2:T(8,128)} %copy.100, f32[256,64,64]{2,1,0:T(8,128)} %copy.87), kind=kOutput, calls=%fused_computation.166 | convolution fusion | flops 805306368 | bytes 12582912 | tf_op jit(solution)/shard_map/xmn,nyx->myx/dot_general | solution.py:65
  (52 shorter events, 189.0 us)
Async XLA Ops:
  13.6 54.0 %all-to-all-start = ((f32[64,64,256]{2,1,0:T(8,128)}), f32[64,64,256]{2,1,0:T(8,128)}, u32[]{:S(2)}, u32[]{:S(2)}) async-start(f32[64,64,256]{2,1,0:T(8,128)} %copy.76), calls=%async_computation | async-start | bytes 8388608 | tf_op jit(solution)/shard_map/all_to_all | solution.py:50
  245.9 19.8 %copy-start.2 = (f32[16,128,512]{2,1,0:T(8,128)S(1)}, f32[16,128,512]{2,1,0:T(8,128)}, u32[]{:S(2)}) copy-start(f32[16,128,512]{2,1,0:T(8,128)} %param.6) | copy-start | bytes 12582916
  287.1 96.8 %all-to-all-start.2 = ((f32[16,512,128]{2,0,1:T(8,128)}), f32[16,512,128]{2,0,1:T(8,128)}, u32[]{:S(2)}, u32[]{:S(2)}) async-start(f32[16,512,128]{2,0,1:T(8,128)} %copy.82), calls=%async_computation.2 | async-start | bytes 8388608 | tf_op jit(solution)/shard_map/all_to_all | solution.py:56
  415.5 53.3 %all-to-all-start.3 = ((f32[4,16,64,256]{3,2,1,0:T(8,128)}), f32[4,16,64,256]{3,2,1,0:T(8,128)}, u32[]{:S(2)}, u32[]{:S(2)}) async-start(f32[4,16,64,256]{3,2,1,0:T(8,128)} %pad_maximum_fusion), calls=%async_computation.3 | async-start | bytes 8388608 | tf_op jit(solution)/shard_map/all_to_all | solution.py:59
  528.8 4.0 copy-start
  537.2 53.3 %all-to-all-start.4 = ((f32[64,64,256]{2,1,0:T(8,128)}), f32[64,64,256]{2,1,0:T(8,128)}, u32[]{:S(2)}, u32[]{:S(2)}) async-start(f32[64,64,256]{2,1,0:T(8,128)} %copy.90), calls=%async_computation.4 | async-start | bytes 8388608 | tf_op jit(solution)/shard_map/all_to_all | solution.py:50
  766.0 19.8 %copy-start.3 = (f32[16,128,512]{2,1,0:T(8,128)S(1)}, f32[16,128,512]{2,1,0:T(8,128)}, u32[]{:S(2)}) copy-start(f32[16,128,512]{2,1,0:T(8,128)} %param.6) | copy-start | bytes 12582916
  807.1 96.9 %all-to-all-start.6 = ((f32[16,512,128]{2,0,1:T(8,128)}), f32[16,512,128]{2,0,1:T(8,128)}, u32[]{:S(2)}, u32[]{:S(2)}) async-start(f32[16,512,128]{2,0,1:T(8,128)} %copy.96), calls=%async_computation.6 | async-start | bytes 8388608 | tf_op jit(solution)/shard_map/all_to_all | solution.py:56
  933.2 51.3 %copy-start.1 = (f32[64,64,256]{2,0,1:T(8,128)S(1)}, f32[64,64,256]{2,0,1:T(8,128)}, u32[]{:S(2)}) copy-start(f32[64,64,256]{2,0,1:T(8,128)} %copy-done) | copy-start | bytes 12582916
  933.2 51.3 %copy-start.4 = (f32[64,64,256]{2,1,0:T(8,128)S(1)}, f32[64,64,256]{2,1,0:T(8,128)}, u32[]{:S(2)}) copy-start(f32[64,64,256]{2,1,0:T(8,128)} %param.5) | copy-start | bytes 12582916
